TPU v7x, 32 devices: a whole 2x2x4 slice. The times are simulated.
32 devices in a mesh: grp: 2 (over core), tp: 4 (over y, x), src: 4 (over z).
Axes of the slice: x: 2, y: 2, z: 4, core: 2. Of those that a mesh axis runs over, the one named last changes fastest.
Arguments:
- hidden_in: bfloat16 [512, 5120], P(('grp', 'src')), may hold values from -6 to 6
- attn_gain: float32 [5120], replicated, may hold values from 0.5 to 1.5
- w_qkv: int32 [1280, 5120], P(None, 'tp'), may hold values from -2147483648 to 2147483646
- qkv_scale: float32 [5120], P('tp'), may hold values from 0.0001118034 to 0.00041926274
- q_gain: float32 [128], replicated, may hold values from 0.25 to 1.75
- k_gain: float32 [128], replicated, may hold values from 0.1 to 1.9
- key_cache: bfloat16 [8, 64, 128, 512], P(('grp', 'src'), 'tp'), may hold values from -400 to 400
- value_cache: bfloat16 [8, 64, 128, 512], P(('grp', 'src'), 'tp'), may hold values from -9 to 9
- lengths: int32 [8, 64], P(('grp', 'src'), 'tp'), may hold values from 1 to 128, as said below
- w_out: int32 [1024, 5120], P('tp'), may hold values from -2147483648 to 2147483646
- out_scale: float32 [5120], replicated, may hold values from 0.0003125 to 0.00125
- mlp_gain: float32 [5120], replicated, may hold values from 0.5 to 1.5
- w_gate: int32 [1280, 12800], P(('grp', 'src'), 'tp'), may hold values from -2147483648 to 2147483646
- w_up: int32 [1280, 12800], P(('grp', 'src'), 'tp'), may hold values from -2147483648 to 2147483646
- gate_scale: float32 [12800], P('tp'), may hold values from 0.0001118034 to 0.00041926274
- up_scale: float32 [12800], P('tp'), may hold values from 0.0001118034 to 0.00041926274
- w_down: int32 [3200, 5120], P('tp', ('grp', 'src')), may hold values from -2147483648 to 2147483646
- down_scale: float32 [5120], replicated, may hold values from 0.00013258251 to 0.00053033006
Outputs:
- layer_out: bfloat16 [512, 5120], P(('grp', 'src'), 'tp')
Inputs may be any that keep to these rules, and one draw needn't show every extreme that they name: `lengths`: some sequence has exactly 128 cached positions.
All inputs are finite; a program needn't handle non-finite values.
Results may differ from a plain program's by a relative error of at most 0.028.
Values may be sent and summed in bfloat16 or wider, within the bound.
A program may use at most 128 MiB of HBM per device.

v0:
```python
import math
import jax
import jax.numpy as jnp
from jax import lax
from jax.sharding import PartitionSpec as P

D = 5120
QUERY_HEADS = 32
KEY_VALUE_HEADS = 4
HEAD_SIZE = 128
QUERY_COLUMNS = 4096
KEY_COLUMNS = 512
norm_epsilon = 1e-06
rope_base = 1000000.0


def unpack_bytes(packed, byte_index):
    return jnp.right_shift(jnp.left_shift(packed, 24 - 8 * byte_index), 24)


def byte_product(activations, packed):
    products = [
        jnp.dot(
            activations[:, byte_index::4],
            unpack_bytes(packed, byte_index).astype(jnp.bfloat16),
            preferred_element_type=jnp.float32,
        )
        for byte_index in range(4)
    ]
    return products[0] + products[1] + products[2] + products[3]


def normalize_rows(values, gain_row):
    return (
        values
        * lax.rsqrt(jnp.mean(values * values, axis=-1, keepdims=True) + norm_epsilon)
        * gain_row
    )


def rotary_embed(values, positions):
    half_dim = values.shape[-1] // 2
    freq_index = jnp.arange(half_dim, dtype=jnp.float32)
    inverse = jnp.exp(freq_index * (-math.log(rope_base) / half_dim))
    angles = positions.astype(jnp.float32)[:, None] * inverse[None, :]
    cosine = jnp.cos(angles)[:, None, :]
    sine_part = jnp.sin(angles)[:, None, :]
    lower_half = values[..., :half_dim]
    upper_half = values[..., half_dim:]
    return jnp.concatenate(
        [
            lower_half * cosine - upper_half * sine_part,
            upper_half * cosine + lower_half * sine_part,
        ],
        axis=-1,
    )


def local_attention(query_key_value_rows, q_gain, k_gain, stored_keys, stored_values, seq_lengths):
    count_of_rows = query_key_value_rows.shape[0]
    cache_length = stored_keys.shape[1]
    query_matrix = (
        query_key_value_rows[:, :QUERY_COLUMNS]
        .astype(jnp.float32)
        .reshape(count_of_rows, QUERY_HEADS, HEAD_SIZE)
    )
    incoming_keys = (
        query_key_value_rows[:, QUERY_COLUMNS : QUERY_COLUMNS + KEY_COLUMNS]
        .astype(jnp.float32)
        .reshape(count_of_rows, KEY_VALUE_HEADS, HEAD_SIZE)
    )
    incoming_values = query_key_value_rows[:, QUERY_COLUMNS + KEY_COLUMNS :].reshape(
        count_of_rows, KEY_VALUE_HEADS, HEAD_SIZE
    )
    query_matrix = rotary_embed(normalize_rows(query_matrix, q_gain), seq_lengths).astype(
        jnp.bfloat16
    )
    incoming_keys = rotary_embed(normalize_rows(incoming_keys, k_gain), seq_lengths).astype(
        jnp.bfloat16
    )
    query_groups = query_matrix.reshape(
        count_of_rows, KEY_VALUE_HEADS, QUERY_HEADS // KEY_VALUE_HEADS, HEAD_SIZE
    )
    key_slices = stored_keys.reshape(count_of_rows, cache_length, KEY_VALUE_HEADS, HEAD_SIZE)
    value_slices = stored_values.reshape(count_of_rows, cache_length, KEY_VALUE_HEADS, HEAD_SIZE)
    logit_scale = 1.0 / math.sqrt(HEAD_SIZE)
    scores = (
        jnp.einsum("bkgd,bpkd->bkgp", query_groups, key_slices, preferred_element_type=jnp.float32)
        * logit_scale
    )
    live_mask = jnp.arange(cache_length, dtype=jnp.int32)[None, :] < seq_lengths[:, None]
    scores = jnp.where(live_mask[:, None, None, :], scores, -jnp.inf)
    self_score = (
        jnp.einsum("nufi,nui->nuf", query_groups, incoming_keys, preferred_element_type=jnp.float32)
        * logit_scale
    )
    row_max = jnp.maximum(jnp.max(scores, axis=-1), self_score)
    soft_weights = jnp.exp(scores - row_max[..., None])
    own_weight = jnp.exp(self_score - row_max)
    denominator = jnp.sum(soft_weights, axis=-1) + own_weight
    own_low = lax.optimization_barrier(own_weight.astype(jnp.bfloat16)).astype(jnp.float32)
    numerator = jnp.einsum(
        "bkgp,bpkd->bkgd",
        soft_weights.astype(jnp.bfloat16),
        value_slices,
        preferred_element_type=jnp.float32,
    )
    numerator = numerator + own_low[..., None] * incoming_values.astype(jnp.float32)[:, :, None, :]
    return (
        (numerator / denominator[..., None])
        .reshape(count_of_rows, QUERY_COLUMNS)
        .astype(jnp.bfloat16)
    )


def local(
    hidden_in,
    attn_gain,
    w_qkv,
    qkv_scale,
    q_gain,
    k_gain,
    key_cache,
    value_cache,
    lengths,
    w_out,
    out_scale,
    mlp_gain,
    w_gate,
    w_up,
    gate_scale,
    up_scale,
    w_down,
    down_scale,
):
    tp_count = lax.axis_size("tp")
    tp_index = lax.axis_index("tp")
    share_cols = D // tp_count
    residual = hidden_in.astype(jnp.float32)
    normed = normalize_rows(residual, attn_gain).astype(jnp.bfloat16)
    qkv_part = (byte_product(normed, w_qkv) * qkv_scale).astype(jnp.bfloat16)
    query_key_value_rows = lax.all_to_all(qkv_part, "tp", split_axis=0, concat_axis=1, tiled=True)
    heads_out = local_attention(
        query_key_value_rows, q_gain, k_gain, key_cache[0], value_cache[0], lengths[0]
    )
    head_rows = lax.all_to_all(heads_out, "tp", split_axis=1, concat_axis=0, tiled=True)
    partial_value = byte_product(head_rows, w_out) * out_scale
    attn_full = lax.psum(partial_value.astype(jnp.bfloat16), "tp").astype(jnp.float32)
    mid_full = (residual + attn_full).astype(jnp.bfloat16)
    normed_mlp = normalize_rows(mid_full.astype(jnp.float32), mlp_gain).astype(jnp.bfloat16)
    mid_share = lax.dynamic_slice_in_dim(mid_full, tp_index * share_cols, share_cols, 1)
    gate_total = byte_product(
        normed_mlp, lax.all_gather(w_gate, ("grp", "src"), axis=0, tiled=True)
    )
    up_total = byte_product(normed_mlp, lax.all_gather(w_up, ("grp", "src"), axis=0, tiled=True))
    activated = (jax.nn.silu(gate_total * gate_scale) * (up_total * up_scale)).astype(jnp.bfloat16)
    down_terms = (
        byte_product(activated, lax.all_gather(w_down, ("grp", "src"), axis=1, tiled=True))
        * down_scale
    )
    mlp_share = lax.psum_scatter(
        down_terms.astype(jnp.bfloat16), "tp", scatter_dimension=1, tiled=True
    ).astype(jnp.float32)
    return (mid_share.astype(jnp.float32) + mlp_share).astype(jnp.bfloat16)


def solution(mesh):
    return jax.shard_map(
        local,
        mesh=mesh,
        in_specs=(
            P(("grp", "src"), None),
            P(),
            P(None, "tp"),
            P("tp"),
            P(),
            P(),
            P(("grp", "src"), "tp", None, None),
            P(("grp", "src"), "tp", None, None),
            P(("grp", "src"), "tp"),
            P("tp", None),
            P(),
            P(),
            P(("grp", "src"), "tp"),
            P(("grp", "src"), "tp"),
            P("tp"),
            P("tp"),
            P("tp", ("grp", "src")),
            P(),
        ),
        out_specs=P(("grp", "src"), "tp"),
        check_vma=False,
    )
```

profile of v0, /device:TPU:0, one launch (start us, length us, event | category | flops | bytes accessed | tf_op | source)
XLA Modules:
  0.0 582.0 jit_solution(6829318386932394782)
XLA Ops:
  7.4 1.3 fusion.81
  8.7 1.3 fusion.83
  10.0 6.5 %slice.73 = bf16[64,1280]{1,0:T(8,128)(2,1)S(1)} slice(bf16[64,5120]{1,0:T(8,128)(2,1)S(1)} %fusion.83), slice={[0:64:1], [0:5120:4]} | slice | bytes 327680 | tf_op jit(solution)/shard_map/slice | solution.py:24
  16.6 6.6 %slice.74 = bf16[64,1280]{1,0:T(8,128)(2,1)S(1)} slice(bf16[64,5120]{1,0:T(8,128)(2,1)S(1)} %fusion.83), slice={[0:64:1], [1:5120:4]} | slice | bytes 327680 | tf_op jit(solution)/shard_map/slice | solution.py:24
  23.1 6.5 %slice.75 = bf16[64,1280]{1,0:T(8,128)(2,1)S(1)} slice(bf16[64,5120]{1,0:T(8,128)(2,1)S(1)} %fusion.83), slice={[0:64:1], [2:5120:4]} | slice | bytes 327680 | tf_op jit(solution)/shard_map/slice | solution.py:24
  29.6 6.7 %slice.76 = bf16[64,1280]{1,0:T(8,128)(2,1)S(1)} slice(bf16[64,5120]{1,0:T(8,128)(2,1)S(1)} %fusion.83), slice={[0:64:1], [3:5120:4]} | slice | bytes 327680 | tf_op jit(solution)/shard_map/slice | solution.py:24
  36.4 4.0 fusion.50
  40.4 0.7 copy-done.1
  41.1 1.0 fusion.71
  42.2 1.0 fusion.70
  43.2 1.5 fusion.73
  44.8 5.3 all-to-all-start
  50.1 2.6 reshape_squeeze.6
  52.7 4.0 reshape_squeeze.7
  56.7 0.1 multiply_cosine_fusion
  57.1 0.1 multiply_reduce_fusion
  57.4 0.1 multiply_multiply_fusion
  57.5 0.1 subtract_convert_fusion.1
  57.6 0.1 fusion.103
  57.9 0.3 fusion.106
  58.1 1.3 fusion.148
  59.5 0.3 fusion.100
  59.9 2.3 fusion.97
  62.3 9.2 %all_to_all.35 = bf16[16,4,1024]{2,0,1:T(8,128)(2,1)S(1)} all-to-all(bf16[16,4,1024]{2,0,1:T(8,128)(2,1)S(1)} %copy.28), channel_id=1, replica_groups=mesh['grp'=2,'tp'=4,'src'=4] {'tp'}, dimensions={1} | all-to-all | bytes 262144 | tf_op jit(solution)/shard_map/all_to_all | solution.py:146
  71.5 1.1 slice.84
  72.7 1.1 slice.85
  73.8 1.1 slice.86
  75.0 1.1 slice.87
  76.1 3.5 fusion.61
  79.6 3.5 convolution_add_fusion.2
  83.1 0.9 convolution_add_fusion.1
  84.0 1.6 fusion.39
  85.7 0.5 all-gather.4.cloned.1.call-update
  86.3 0.5 all-gather.6.cloned.1.call-update
  86.9 0.5 all-gather.8.cloned.1.call-update
  87.5 44.9 %all-reduce.2.cloned.1.call-done = bf16[64,5120]{1,0:T(8,128)(2,1)} async-done(((bf16[64,5120]{1,0:T(8,128)(2,1)}), bf16[64,5120]{1,0:T(8,128)(2,1)}) %all-reduce.2.cloned.1.call-update) | async-done | bytes 655376 | tf_op jit(solution)/shard_map/psum | solution.py:148
  132.4 1.4 fusion.78
  133.8 0.2 fusion.80
  134.0 7.0 %slice.88 = bf16[64,1280]{1,0:T(8,128)(2,1)S(1)} slice(bf16[64,5120]{1,0:T(8,128)(2,1)S(1)} %fusion.80), slice={[0:64:1], [0:5120:4]} | slice | bytes 327680 | tf_op jit(solution)/shard_map/slice | solution.py:24
  141.0 6.6 %slice.89 = bf16[64,1280]{1,0:T(8,128)(2,1)S(1)} slice(bf16[64,5120]{1,0:T(8,128)(2,1)S(1)} %fusion.80), slice={[0:64:1], [1:5120:4]} | slice | bytes 327680 | tf_op jit(solution)/shard_map/slice | solution.py:24
  147.6 6.5 %slice.90 = bf16[64,1280]{1,0:T(8,128)(2,1)S(1)} slice(bf16[64,5120]{1,0:T(8,128)(2,1)S(1)} %fusion.80), slice={[0:64:1], [2:5120:4]} | slice | bytes 327680 | tf_op jit(solution)/shard_map/slice | solution.py:24
  154.1 6.7 %slice.91 = bf16[64,1280]{1,0:T(8,128)(2,1)S(1)} slice(bf16[64,5120]{1,0:T(8,128)(2,1)S(1)} %fusion.80), slice={[0:64:1], [3:5120:4]} | slice | bytes 327680 | tf_op jit(solution)/shard_map/slice | solution.py:24
  160.8 74.5 %all-gather.4.cloned.1.call-done = s32[1280,3200]{1,0:T(8,128)} async-done(((s32[160,3200]{1,0:T(8,128)}), s32[1280,3200]{1,0:T(8,128)}) %all-gather.4.cloned.1.call-update) | async-done | bytes 16384016 | tf_op jit(solution)/shard_map/all_gather | solution.py:153
  235.3 8.0 %fusion = f32[64,3200]{1,0:T(8,128)S(1)} fusion(bf16[64,1280]{1,0:T(8,128)(2,1)S(1)} %slice.88, s32[1280,3200]{1,0:T(8,128)} %all-gather.4.cloned.1.call-done), kind=kOutput, calls=%fused_computation.12 | convolution fusion | flops 536576000 | bytes 17367040 | tf_op jit(solution)/shard_map/dot_general | solution.py:23
  243.3 139.4 %all-gather.6.cloned.1.call-done = s32[1280,3200]{1,0:T(8,128)} async-done(((s32[160,3200]{1,0:T(8,128)}), s32[1280,3200]{1,0:T(8,128)}) %all-gather.6.cloned.1.call-update) | async-done | bytes 16384016 | tf_op jit(solution)/shard_map/all_gather | solution.py:155
  382.7 8.1 %fusion.4 = f32[64,3200]{1,0:T(8,128)S(1)} fusion(bf16[64,1280]{1,0:T(8,128)(2,1)S(1)} %slice.88, s32[1280,3200]{1,0:T(8,128)} %all-gather.6.cloned.1.call-done), kind=kOutput, calls=%fused_computation.16 | convolution fusion | flops 536576000 | bytes 17367040 | tf_op jit(solution)/shard_map/dot_general | solution.py:23
  390.8 9.9 %fusion.45 = f32[64,3200]{1,0:T(8,128)S(1)} fusion(f32[64,3200]{1,0:T(8,128)S(1)} %fusion, bf16[64,1280]{1,0:T(8,128)(2,1)S(1)} %slice.89, s32[1280,3200]{1,0:T(8,128)} %all-gather.4.cloned.1.call-done), kind=kOutput, calls=%fused_computation.68 | convolution fusion | flops 536780800 | bytes 18186240 | tf_op jit(solution)/shard_map/dot_general | solution.py:23
  400.8 2.4 fusion.42
  403.2 8.0 %fusion.44 = f32[64,3200]{1,0:T(8,128)S(1)} fusion(f32[64,3200]{1,0:T(8,128)S(1)} %fusion.45, bf16[64,1280]{1,0:T(8,128)(2,1)S(1)} %slice.90, s32[1280,3200]{1,0:T(8,128)} %all-gather.4.cloned.1.call-done), kind=kOutput, calls=%fused_computation.67 | convolution fusion | flops 536780800 | bytes 18186240 | tf_op jit(solution)/shard_map/dot_general | solution.py:23
  411.2 2.6 fusion.41
  413.9 7.6 %fusion.46 = f32[64,3200]{1,0:T(8,128)S(1)} fusion(f32[64,3200]{1,0:T(8,128)S(1)} %fusion.44, bf16[64,1280]{1,0:T(8,128)(2,1)S(1)} %slice.91, s32[1280,3200]{1,0:T(8,128)} %all-gather.4.cloned.1.call-done, f32[3200]{0:T(1024)S(1)} %copy-done.7), kind=kOutput, calls=%fused_computation.69 | convolution fusion | flops 536985600 | bytes 18199040 | tf_op jit(solution)/shard_map/dot_general | solution.py:23
  421.5 2.0 fusion.49
  423.5 3.7 slice.92
  427.2 3.7 slice.93
  430.9 3.7 slice.94
  434.6 4.0 slice.95
  438.6 91.5 %all-gather.8.cloned.1.call-done = s32[800,5120]{1,0:T(8,128)} async-done(((s32[800,640]{1,0:T(8,128)}), s32[800,5120]{1,0:T(8,128)}) %all-gather.8.cloned.1.call-update) | async-done | bytes 16384016 | tf_op jit(solution)/shard_map/all_gather | solution.py:158
  530.1 8.2 %fusion.8 = f32[64,5120]{1,0:T(8,128)S(1)} fusion(bf16[64,800]{1,0:T(8,128)(2,1)S(1)} %slice.92, s32[800,5120]{1,0:T(8,128)} %all-gather.8.cloned.1.call-done), kind=kOutput, calls=%fused_computation.20 | convolution fusion | flops 536576000 | bytes 17797120 | tf_op jit(solution)/shard_map/dot_general | solution.py:23
  538.3 2.1 copy-done
  540.4 2.5 fusion.36
  542.9 2.5 fusion.35
  545.4 2.9 fusion.38
  548.3 24.0 %reduce-scatter.2.cloned.1.call-done = bf16[64,1280]{1,0:T(8,128)(2,1)} async-done(((bf16[64,5120]{1,0:T(8,128)(2,1)}), bf16[64,1280]{1,0:T(8,128)(2,1)}) %reduce-scatter.2.cloned.1.call-update) | async-done | bytes 163856 | tf_op jit(solution)/shard_map/reduce_scatter | solution.py:161
  572.3 1.6 add_convert_fusion
  (65 shorter events, 0.9 us)
Async XLA Ops:
  36.4 4.7 copy-start.1
  41.1 2.1 copy-start.8
  42.2 8.0 %copy-start.11 = (s32[1,16]{1,0:T(1,128)S(1)}, s32[1,16]{1,0:T(1,128)}, u32[]{:S(2)}) copy-start(s32[1,16]{1,0:T(1,128)} %param.26) | copy-start | bytes 196
  44.8 12.5 %copy-start.9 = (f32[128]{0:T(128)S(1)}, f32[128]{0:T(128)}, u32[]{:S(2)}) copy-start(f32[128]{0:T(128)} %param.23) | copy-start | bytes 1540
  44.8 12.6 %copy-start.10 = (f32[128]{0:T(128)S(1)}, f32[128]{0:T(128)}, u32[]{:S(2)}) copy-start(f32[128]{0:T(128)} %param.22) | copy-start | bytes 1540
  44.8 12.1 %all-to-all-start = ((bf16[4,16,1280]{2,1,0:T(8,128)(2,1)}), bf16[4,16,1280]{2,1,0:T(8,128)(2,1)S(1)}, u32[]{:S(2)}, u32[]{:S(2)}) async-start(bf16[4,16,1280]{2,1,0:T(8,128)(2,1)} %bitcast.1), calls=%async_computation | async-start | bytes 327680 | tf_op jit(solution)/shard_map/all_to_all | solution.py:142
  50.1 82.3 %all-reduce.2.cloned.1.call-start = ((), (), s32[]{:S(2)}) async-start(), calls=%async_computation.3 | async-start | bytes 1310720 | tf_op jit(solution)/shard_map/psum | solution.py:148
  76.1 7.0 %slice-start.4 = ((s8[5242880]{0:T(1024)(128)(4,1)}), s8[4194304]{0:T(1024)(128)(4,1)S(1)}, s32[]{:S(2)}) async-start(s8[5242880]{0:T(1024)(128)(4,1)} %bitcast.49), calls=%async_computation.12 | async-start | bytes 8388608
  79.6 3.5 slice-start.5
  79.6 4.4 copy-start.4
  84.0 48.3 %copy-start.2 = (bf16[64,5120]{1,0:T(8,128)(2,1)S(1)}, bf16[64,5120]{1,0:T(8,128)(2,1)}, u32[]{:S(2)}) copy-start(bf16[64,5120]{1,0:T(8,128)(2,1)} %param.18) | copy-start | bytes 1966084
  84.0 49.8 %copy-start.5 = (f32[5120]{0:T(1024)S(1)}, f32[5120]{0:T(1024)}, u32[]{:S(2)}) copy-start(f32[5120]{0:T(1024)} %param.29) | copy-start | bytes 61444
  85.7 149.6 %all-gather.4.cloned.1.call-start = ((), (), s32[]{:S(2)}) async-start(), calls=%async_computation.4 | async-start | bytes 18432000 | tf_op jit(solution)/shard_map/all_gather | solution.py:153
  86.3 296.4 %all-gather.6.cloned.1.call-start = ((), (), s32[]{:S(2)}) async-start(), calls=%async_computation.5 | async-start | bytes 18432000 | tf_op jit(solution)/shard_map/all_gather | solution.py:155
  86.9 443.2 %all-gather.8.cloned.1.call-start = ((), (), s32[]{:S(2)}) async-start(), calls=%async_computation.6 | async-start | bytes 18432000 | tf_op jit(solution)/shard_map/all_gather | solution.py:158
  87.4 484.9 %reduce-scatter.2.cloned.1.call-start = ((), (), s32[]{:S(2)}) async-start(), calls=%async_computation.7 | async-start | bytes 819200 | tf_op jit(solution)/shard_map/reduce_scatter | solution.py:161
  382.7 18.1 %slice-start = ((s8[16384000]{0:T(1024)(128)(4,1)}), s8[4194304]{0:T(1024)(128)(4,1)S(1)}, s32[]{:S(2)}) async-start(s8[16384000]{0:T(1024)(128)(4,1)} %bitcast.47), calls=%async_computation.8 | async-start | bytes 8388608
  382.7 18.1 %slice-start.1 = ((s8[16384000]{0:T(1024)(128)(4,1)}), s8[4194304]{0:T(1024)(128)(4,1)S(1)}, s32[]{:S(2)}) async-start(s8[16384000]{0:T(1024)(128)(4,1)} %bitcast.47), calls=%async_computation.9 | async-start | bytes 8388608
  390.8 9.9 %slice-start.2 = ((s8[16384000]{0:T(1024)(128)(4,1)}), s8[4194304]{0:T(1024)(128)(4,1)S(1)}, s32[]{:S(2)}) async-start(s8[16384000]{0:T(1024)(128)(4,1)} %bitcast.47), calls=%async_computation.10 | async-start | bytes 8388608
  390.8 9.9 %slice-start.3 = ((s8[16384000]{0:T(1024)(128)(4,1)}), s8[3801088]{0:T(1024)(128)(4,1)S(1)}, s32[]{:S(2)}) async-start(s8[16384000]{0:T(1024)(128)(4,1)} %bitcast.47), calls=%async_computation.11 | async-start | bytes 7602176
  411.2 2.6 copy-start.7
  413.9 7.6 %copy-start.6 = (f32[3200]{0:T(1024)S(1)}, f32[3200]{0:T(1024)}, u32[]{:S(2)}) copy-start(f32[3200]{0:T(1024)} %param.33) | copy-start | bytes 38404
  530.1 10.3 %copy-start = (s32[800,5120]{1,0:T(8,128)S(1)}, s32[800,5120]{1,0:T(8,128)}, u32[]{:S(2)}) copy-start(s32[800,5120]{1,0:T(8,128)} %all-gather.8.cloned.1.call-done) | copy-start | bytes 49152004
  542.9 2.5 copy-start.3
Sparse Core Ops, SparseCore 0:
  85.8 46.4 all-reduce.1
  548.4 23.8 reduce-scatter.1
Sparse Core Ops, SparseCore 1:
  87.8 147.4 all-gather.3
  236.7 145.9 all-gather.5
  384.2 145.9 all-gather.7
where the time goes:
time: 589 us; the launch traced here: 582 us
  waiting for transfers between devices  376 us (64%)
  matrix products  85.7 us (15%)
  local copies, waits for them, and re-layouts  82.3 us (14%)
  between operations  16.1 us (3%)
  blocking collectives  9.25 us (2%)
  other arithmetic  7.26 us (1%)
    all_gather x1, waiting for transfers between devices, local(): lax.all_gather(w_up, ('grp', 'src'), axis=0, tiled=True)  139 us
    all_gather x1, waiting for transfers between devices, local(): lax.all_gather(w_down, ('grp', 'src'), axis=1, tiled=True)  91.5 us
    dot_general x20, matrix products, byte_product(): jnp.dot(activations[:, byte_index::4], unpack_bytes(packed, byte_index).a...  81.8 us
    all_gather x1, waiting for transfers between devices, local(): lax.all_gather(w_gate, ('grp', 'src'), axis=0, tiled=True)  74.5 us
    slice x16, local copies, waits for them, and re-layouts, byte_product(): activations[:, byte_index::4]  72.7 us
    psum x1, waiting for transfers between devices, local(): lax.psum(partial_value.astype(jnp.bfloat16), 'tp').astype(jnp.float32)  44.9 us
    reduce_scatter x1, waiting for transfers between devices, local(): lax.psum_scatter(down_terms.astype(jnp.bfloat16), 'tp', scatter_dimension...  24 us
  transfers between devices with their start and end apart: 6, of which 5 were waited for; matrix products, arithmetic and copies ran while one was open for 17% of the time, Pallas kernels for 0%

commit v1 on v0

--- a/solution.py
+++ b/solution.py
@@ -155,7 +155,7 @@
     up_total = byte_product(normed_mlp, lax.all_gather(w_up, ("grp", "src"), axis=0, tiled=True))
     activated = (jax.nn.silu(gate_total * gate_scale) * (up_total * up_scale)).astype(jnp.bfloat16)
     down_terms = (
-        byte_product(activated, lax.all_gather(w_down, ("grp", "src"), axis=1, tiled=True))
+        byte_product(activated, jnp.concatenate(lax.all_gather(w_down, ("grp", "src")), axis=1))
         * down_scale
     )
     mlp_share = lax.psum_scatter(

time: 589 us -> 626 us (1.063)
  local copies, waits for them, and re-layouts: 82.3 us -> 109 us
  other arithmetic: 7.26 us -> 24.4 us
    unnamed x37 -> x51, local copies, waits for them, and re-layouts: 2.96 us -> 28 us
    convert_element_type x0 -> x1, other arithmetic: none -> 17 us  [byte_product(): unpack_bytes(packed, byte_index).astype(jnp.bfloat16)]
  transfers between devices with their start and end apart: 6 -> 6, of which waited for: 5 -> 5; matrix products, arithmetic and copies ran while one was open for 17% -> 16% of each run, Pallas kernels for 0% -> 0%
where the time goes in v1:
time: 626 us; the launch traced here: 619 us
  waiting for transfers between devices  374 us (60%)
  local copies, waits for them, and re-layouts  109 us (17%)
  matrix products  80.9 us (13%)
  other arithmetic  24.4 us (4%)
  between operations  16.1 us (3%)
  blocking collectives  9.25 us (1%)
    all_gather x1, waiting for transfers between devices, local(): lax.all_gather(w_up, ('grp', 'src'), axis=0, tiled=True)  139 us
    all_gather x1, waiting for transfers between devices, local(): lax.all_gather(w_down, ('grp', 'src'))  90.1 us
    dot_general x20, matrix products, byte_product(): jnp.dot(activations[:, byte_index::4], unpack_bytes(packed, byte_index).a...  77 us
    slice x16, local copies, waits for them, and re-layouts, byte_product(): activations[:, byte_index::4]  74.2 us
    all_gather x1, waiting for transfers between devices, local(): lax.all_gather(w_gate, ('grp', 'src'), axis=0, tiled=True)  73.6 us
    psum x1, waiting for transfers between devices, local(): lax.psum(partial_value.astype(jnp.bfloat16), 'tp').astype(jnp.float32)  44.9 us
    unnamed x51, local copies, waits for them, and re-layouts  28 us
    reduce_scatter x1, waiting for transfers between devices, local(): lax.psum_scatter(down_terms.astype(jnp.bfloat16), 'tp', scatter_dimension...  24 us
  transfers between devices with their start and end apart: 6, of which 5 were waited for; matrix products, arithmetic and copies ran while one was open for 16% of the time, Pallas kernels for 0%

profile of v1, /device:TPU:0, one launch (start us, length us, event | category | flops | bytes accessed | tf_op | source)
XLA Modules:
  0.0 618.5 jit_solution(15865815261883425891)
XLA Ops:
  7.4 1.3 fusion.67
  8.7 1.3 fusion.69
  10.0 6.5 %slice.73 = bf16[64,1280]{1,0:T(8,128)(2,1)S(1)} slice(bf16[64,5120]{1,0:T(8,128)(2,1)S(1)} %fusion.69), slice={[0:64:1], [0:5120:4]} | slice | bytes 327680 | tf_op jit(solution)/shard_map/slice | solution.py:24
  16.6 6.6 %slice.74 = bf16[64,1280]{1,0:T(8,128)(2,1)S(1)} slice(bf16[64,5120]{1,0:T(8,128)(2,1)S(1)} %fusion.69), slice={[0:64:1], [1:5120:4]} | slice | bytes 327680 | tf_op jit(solution)/shard_map/slice | solution.py:24
  23.1 6.5 %slice.75 = bf16[64,1280]{1,0:T(8,128)(2,1)S(1)} slice(bf16[64,5120]{1,0:T(8,128)(2,1)S(1)} %fusion.69), slice={[0:64:1], [2:5120:4]} | slice | bytes 327680 | tf_op jit(solution)/shard_map/slice | solution.py:24
  29.6 6.7 %slice.76 = bf16[64,1280]{1,0:T(8,128)(2,1)S(1)} slice(bf16[64,5120]{1,0:T(8,128)(2,1)S(1)} %fusion.69), slice={[0:64:1], [3:5120:4]} | slice | bytes 327680 | tf_op jit(solution)/shard_map/slice | solution.py:24
  36.4 4.0 fusion.36
  40.4 0.7 copy-done
  41.1 1.0 fusion.57
  42.2 1.0 fusion.56
  43.2 1.5 fusion.59
  44.8 5.3 all-to-all-start
  50.1 2.6 reshape_squeeze.6
  52.7 4.0 reshape_squeeze.7
  58.1 1.3 fusion.127
  59.5 0.3 fusion.86
  59.9 2.3 fusion.83
  62.3 9.2 %all_to_all.35 = bf16[16,4,1024]{2,0,1:T(8,128)(2,1)S(1)} all-to-all(bf16[16,4,1024]{2,0,1:T(8,128)(2,1)S(1)} %copy.32), channel_id=1, replica_groups=mesh['grp'=2,'tp'=4,'src'=4] {'tp'}, dimensions={1} | all-to-all | bytes 262144 | tf_op jit(solution)/shard_map/all_to_all | solution.py:146
  71.5 1.1 slice.84
  72.7 1.1 slice.85
  73.8 1.1 slice.86
  75.0 1.1 slice.87
  76.1 3.5 fusion.47
  79.6 3.5 convolution_add_fusion.2
  83.1 0.9 convolution_add_fusion.1
  84.0 1.6 fusion.25
  85.7 0.5 all-gather.5.cloned.1.call-update
  86.3 0.5 all-gather.7.cloned.1.call-update
  86.9 0.5 all-gather.9.cloned.1.call-update
  87.5 44.9 %all-reduce.2.cloned.1.call-done = bf16[64,5120]{1,0:T(8,128)(2,1)} async-done(((bf16[64,5120]{1,0:T(8,128)(2,1)}), bf16[64,5120]{1,0:T(8,128)(2,1)}) %all-reduce.2.cloned.1.call-update) | async-done | bytes 655376 | tf_op jit(solution)/shard_map/psum | solution.py:148
  132.3 1.4 fusion.64
  133.8 0.8 copy-done.3
  134.9 7.0 %slice.88 = bf16[64,1280]{1,0:T(8,128)(2,1)S(1)} slice(bf16[64,5120]{1,0:T(8,128)(2,1)S(1)} %fusion.66), slice={[0:64:1], [0:5120:4]} | slice | bytes 327680 | tf_op jit(solution)/shard_map/slice | solution.py:24
  141.9 6.6 %slice.89 = bf16[64,1280]{1,0:T(8,128)(2,1)S(1)} slice(bf16[64,5120]{1,0:T(8,128)(2,1)S(1)} %fusion.66), slice={[0:64:1], [1:5120:4]} | slice | bytes 327680 | tf_op jit(solution)/shard_map/slice | solution.py:24
  148.4 6.5 %slice.90 = bf16[64,1280]{1,0:T(8,128)(2,1)S(1)} slice(bf16[64,5120]{1,0:T(8,128)(2,1)S(1)} %fusion.66), slice={[0:64:1], [2:5120:4]} | slice | bytes 327680 | tf_op jit(solution)/shard_map/slice | solution.py:24
  154.9 6.7 %slice.91 = bf16[64,1280]{1,0:T(8,128)(2,1)S(1)} slice(bf16[64,5120]{1,0:T(8,128)(2,1)S(1)} %fusion.66), slice={[0:64:1], [3:5120:4]} | slice | bytes 327680 | tf_op jit(solution)/shard_map/slice | solution.py:24
  161.6 73.6 %all-gather.5.cloned.1.call-done = s32[1280,3200]{1,0:T(8,128)} async-done(((s32[160,3200]{1,0:T(8,128)}), s32[1280,3200]{1,0:T(8,128)}) %all-gather.5.cloned.1.call-update) | async-done | bytes 16384016 | tf_op jit(solution)/shard_map/all_gather | solution.py:153
  235.3 8.0 %fusion = f32[64,3200]{1,0:T(8,128)S(1)} fusion(bf16[64,1280]{1,0:T(8,128)(2,1)S(1)} %slice.88, s32[1280,3200]{1,0:T(8,128)} %all-gather.5.cloned.1.call-done), kind=kOutput, calls=%fused_computation.12 | convolution fusion | flops 536576000 | bytes 17367040 | tf_op jit(solution)/shard_map/dot_general | solution.py:23
  243.3 139.4 %all-gather.7.cloned.1.call-done = s32[1280,3200]{1,0:T(8,128)} async-done(((s32[160,3200]{1,0:T(8,128)}), s32[1280,3200]{1,0:T(8,128)}) %all-gather.7.cloned.1.call-update) | async-done | bytes 16384016 | tf_op jit(solution)/shard_map/all_gather | solution.py:155
  382.7 8.1 %fusion.4 = f32[64,3200]{1,0:T(8,128)S(1)} fusion(bf16[64,1280]{1,0:T(8,128)(2,1)S(1)} %slice.88, s32[1280,3200]{1,0:T(8,128)} %all-gather.7.cloned.1.call-done), kind=kOutput, calls=%fused_computation.16 | convolution fusion | flops 536576000 | bytes 17367040 | tf_op jit(solution)/shard_map/dot_general | solution.py:23
  390.8 9.9 %fusion.31 = f32[64,3200]{1,0:T(8,128)S(1)} fusion(f32[64,3200]{1,0:T(8,128)S(1)} %fusion, bf16[64,1280]{1,0:T(8,128)(2,1)S(1)} %slice.89, s32[1280,3200]{1,0:T(8,128)} %all-gather.5.cloned.1.call-done), kind=kOutput, calls=%fused_computation.57 | convolution fusion | flops 536780800 | bytes 18186240 | tf_op jit(solution)/shard_map/dot_general | solution.py:23
  400.8 2.4 fusion.28
  403.2 8.1 %fusion.30 = f32[64,3200]{1,0:T(8,128)S(1)} fusion(f32[64,3200]{1,0:T(8,128)S(1)} %fusion.31, bf16[64,1280]{1,0:T(8,128)(2,1)S(1)} %slice.90, s32[1280,3200]{1,0:T(8,128)} %all-gather.5.cloned.1.call-done), kind=kOutput, calls=%fused_computation.56 | convolution fusion | flops 536780800 | bytes 18186240 | tf_op jit(solution)/shard_map/dot_general | solution.py:23
  411.2 2.6 fusion.27
  413.9 7.6 %fusion.32 = f32[64,3200]{1,0:T(8,128)S(1)} fusion(f32[64,3200]{1,0:T(8,128)S(1)} %fusion.30, bf16[64,1280]{1,0:T(8,128)(2,1)S(1)} %slice.91, s32[1280,3200]{1,0:T(8,128)} %all-gather.5.cloned.1.call-done, f32[3200]{0:T(1024)S(1)} %copy-done.10), kind=kOutput, calls=%fused_computation.58 | convolution fusion | flops 536985600 | bytes 18199040 | tf_op jit(solution)/shard_map/dot_general | solution.py:23
  421.4 2.0 fusion.35
  423.5 4.3 slice.92
  427.8 4.3 slice.93
  432.1 4.3 slice.94
  436.3 3.7 slice.95
  440.0 90.1 %all-gather.9.cloned.1.call-done = s32[6400,640]{1,0:T(8,128)} async-done(((s32[800,640]{1,0:T(8,128)}), s32[6400,640]{1,0:T(8,128)}) %all-gather.9.cloned.1.call-update) | async-done | bytes 16384016 | tf_op jit(solution)/shard_map/all_gather | solution.py:158
  530.1 17.0 %shift-right-arithmetic_convert_fusion = (bf16[6400,640]{1,0:T(8,128)(2,1)}, bf16[6400,640]{1,0:T(8,128)(2,1)S(1)}, bf16[6400,640]{1,0:T(8,128)(2,1)}, bf16[6400,640]{1,0:T(8,128)(2,1)}) fusion(s32[6400,640]{1,0:T(8,128)} %all-gather.9.cloned.1.call-done), kind=kLoop, calls=%fused_computation | loop fusion | flops 49152000 | bytes 49152000 | tf_op jit(solution)/shard_map/convert_element_type | solution.py:25
  547.1 7.9 %copy.41 = bf16[100,8,8,640]{3,1,2,0:T(8,128)(2,1)} copy(bf16[100,8,8,640]{3,1,0,2:T(8,128)(2,1)} %bitcast.88) | data formatting | bytes 16384000
  555.0 7.9 %copy.42 = bf16[100,8,8,640]{3,1,2,0:T(8,128)(2,1)} copy(bf16[100,8,8,640]{3,1,0,2:T(8,128)(2,1)} %bitcast.87) | data formatting | bytes 16384000
  562.9 4.5 copy.43
  567.4 4.7 copy.44
  572.1 5.3 fusion.128
  577.4 0.4 copy-done.1
  577.8 1.7 convolution_add_fusion.5
  579.6 0.9 slice-done.7
  580.4 1.7 convolution_add_fusion.4
  582.2 2.6 fusion.24
  584.8 24.0 %reduce-scatter.2.cloned.1.call-done = bf16[64,1280]{1,0:T(8,128)(2,1)} async-done(((bf16[64,5120]{1,0:T(8,128)(2,1)}), bf16[64,1280]{1,0:T(8,128)(2,1)}) %reduce-scatter.2.cloned.1.call-update) | async-done | bytes 163856 | tf_op jit(solution)/shard_map/reduce_scatter | solution.py:161
  608.8 1.7 add_convert_fusion
  (81 shorter events, 2.1 us)
Async XLA Ops:
  36.4 4.7 copy-start
  41.1 2.1 copy-start.11
  42.2 8.0 %copy-start.14 = (s32[1,16]{1,0:T(1,128)S(1)}, s32[1,16]{1,0:T(1,128)}, u32[]{:S(2)}) copy-start(s32[1,16]{1,0:T(1,128)} %param.26) | copy-start | bytes 196
  44.8 12.5 %copy-start.12 = (f32[128]{0:T(128)S(1)}, f32[128]{0:T(128)}, u32[]{:S(2)}) copy-start(f32[128]{0:T(128)} %param.23) | copy-start | bytes 1540
  44.8 12.6 %copy-start.13 = (f32[128]{0:T(128)S(1)}, f32[128]{0:T(128)}, u32[]{:S(2)}) copy-start(f32[128]{0:T(128)} %param.22) | copy-start | bytes 1540
  44.8 12.1 %all-to-all-start = ((bf16[4,16,1280]{2,1,0:T(8,128)(2,1)}), bf16[4,16,1280]{2,1,0:T(8,128)(2,1)S(1)}, u32[]{:S(2)}, u32[]{:S(2)}) async-start(bf16[4,16,1280]{2,1,0:T(8,128)(2,1)} %bitcast.1), calls=%async_computation | async-start | bytes 327680 | tf_op jit(solution)/shard_map/all_to_all | solution.py:142
  50.1 82.2 %all-reduce.2.cloned.1.call-start = ((), (), s32[]{:S(2)}) async-start(), calls=%async_computation.3 | async-start | bytes 1310720 | tf_op jit(solution)/shard_map/psum | solution.py:148
  76.1 7.0 %slice-start.4 = ((s8[5242880]{0:T(1024)(128)(4,1)}), s8[4194304]{0:T(1024)(128)(4,1)S(1)}, s32[]{:S(2)}) async-start(s8[5242880]{0:T(1024)(128)(4,1)} %bitcast.77), calls=%async_computation.12 | async-start | bytes 8388608
  79.6 3.5 slice-start.5
  79.6 4.4 copy-start.7
  84.0 48.3 %copy-start.2 = (bf16[64,5120]{1,0:T(8,128)(2,1)S(1)}, bf16[64,5120]{1,0:T(8,128)(2,1)}, u32[]{:S(2)}) copy-start(bf16[64,5120]{1,0:T(8,128)(2,1)} %param.18) | copy-start | bytes 1966084
  84.0 50.6 %copy-start.8 = (f32[5120]{0:T(1024)S(1)}, f32[5120]{0:T(1024)}, u32[]{:S(2)}) copy-start(f32[5120]{0:T(1024)} %param.29) | copy-start | bytes 61444
  85.7 149.6 %all-gather.5.cloned.1.call-start = ((), (), s32[]{:S(2)}) async-start(), calls=%async_computation.4 | async-start | bytes 18432000 | tf_op jit(solution)/shard_map/all_gather | solution.py:153
  86.3 296.4 %all-gather.7.cloned.1.call-start = ((), (), s32[]{:S(2)}) async-start(), calls=%async_computation.5 | async-start | bytes 18432000 | tf_op jit(solution)/shard_map/all_gather | solution.py:155
  86.8 443.2 %all-gather.9.cloned.1.call-start = ((), (), s32[]{:S(2)}) async-start(), calls=%async_computation.7 | async-start | bytes 18432000 | tf_op jit(solution)/shard_map/all_gather | solution.py:158
  87.4 521.4 %reduce-scatter.2.cloned.1.call-start = ((), (), s32[]{:S(2)}) async-start(), calls=%async_computation.6 | async-start | bytes 819200 | tf_op jit(solution)/shard_map/reduce_scatter | solution.py:161
  133.8 0.9 copy-start.3
  382.7 18.1 %slice-start = ((s8[16384000]{0:T(1024)(128)(4,1)}), s8[4194304]{0:T(1024)(128)(4,1)S(1)}, s32[]{:S(2)}) async-start(s8[16384000]{0:T(1024)(128)(4,1)} %bitcast.75), calls=%async_computation.8 | async-start | bytes 8388608
  382.7 18.1 %slice-start.1 = ((s8[16384000]{0:T(1024)(128)(4,1)}), s8[4194304]{0:T(1024)(128)(4,1)S(1)}, s32[]{:S(2)}) async-start(s8[16384000]{0:T(1024)(128)(4,1)} %bitcast.75), calls=%async_computation.9 | async-start | bytes 8388608
  390.8 9.9 %slice-start.2 = ((s8[16384000]{0:T(1024)(128)(4,1)}), s8[4194304]{0:T(1024)(128)(4,1)S(1)}, s32[]{:S(2)}) async-start(s8[16384000]{0:T(1024)(128)(4,1)} %bitcast.75), calls=%async_computation.10 | async-start | bytes 8388608
  390.8 9.9 %slice-start.3 = ((s8[16384000]{0:T(1024)(128)(4,1)}), s8[3801088]{0:T(1024)(128)(4,1)S(1)}, s32[]{:S(2)}) async-start(s8[16384000]{0:T(1024)(128)(4,1)} %bitcast.75), calls=%async_computation.11 | async-start | bytes 7602176
  411.2 2.6 copy-start.10
  413.9 7.6 %copy-start.9 = (f32[3200]{0:T(1024)S(1)}, f32[3200]{0:T(1024)}, u32[]{:S(2)}) copy-start(f32[3200]{0:T(1024)} %param.33) | copy-start | bytes 38404
  572.1 5.7 copy-start.1
  572.1 5.7 copy-start.5
  572.1 7.4 %slice-start.6 = ((s8[8192000]{0:T(1024)(128)(4,1)}), s8[4194304]{0:T(1024)(128)(4,1)S(1)}, s32[]{:S(2)}) async-start(s8[8192000]{0:T(1024)(128)(4,1)} %bitcast.81), calls=%async_computation.14 | async-start | bytes 8388608
  577.8 2.6 slice-start.7
  577.8 2.6 copy-start.4
  580.4 1.7 copy-start.6
Sparse Core Ops, SparseCore 0:
  85.8 46.4 all-reduce.1
  584.9 23.8 reduce-scatter.1
Sparse Core Ops, SparseCore 1:
  87.8 147.4 all-gather.4
  236.7 145.9 all-gather.6
  384.1 145.9 all-gather.8
